TPU v7x, 32 devices: a whole 2x2x4 slice. The times are simulated.
32 devices in a mesh: ep: 8 (over z, x), tp: 4 (over y, core).
Axes of the slice: x: 2, y: 2, z: 4, core: 2. Of those that a mesh axis runs over, the one named last changes fastest.
Arguments:
- tokens: bfloat16 [1024, 3072], P('ep', 'tp'), may hold values from -6 to 6
- expert_ids: int32 [1024, 2], P('ep'), may hold values from 0 to 7, all different within a row
- route_share: float32 [1024], P('ep'), may hold values from 0.5 to 0.95
- w_gate: bfloat16 [65536, 3072], P(('ep', 'tp')), may hold values from -0.109375 to 0.109375
- w_up: bfloat16 [65536, 3072], P(('ep', 'tp')), may hold values from -0.109375 to 0.109375
- w_down: bfloat16 [65536, 3072], P(('ep', 'tp')), may hold values from -0.0625 to 0.0625
- reward_head: float32 [3072], P('tp'), may hold values from -0.109375 to 0.109375
- upstream: bfloat16 [1024, 3072], P('ep', 'tp'), may hold values from -4 to 4
- pair_order: int32 [16], replicated, may hold values from 0 to 15, each once
Outputs:
- layer_out: bfloat16 [1024, 3072], P('ep', 'tp')
- rewards: float32 [16], replicated
- pair_loss: float32 [], replicated
- grad_tokens: bfloat16 [1024, 3072], P('ep', 'tp')
- grad_gate: bfloat16 [65536, 3072], P(('ep', 'tp'))
- grad_up: bfloat16 [65536, 3072], P(('ep', 'tp'))
- grad_down: bfloat16 [65536, 3072], P(('ep', 'tp'))
Inputs may be any that keep to these rules, and one draw needn't show every extreme that they name: `expert_ids`: each row names 2 different experts. `pair_order`: each of the 16 sequence indices appears once.
All inputs are finite; a program needn't handle non-finite values.
Results may differ from a plain program's by a relative error of at most 0.014.
Values may be sent and summed in bfloat16 or wider, within the bound.
A program may use at most 128 MiB of HBM per device.

v0:
```python
import math
import jax
import jax.numpy as jnp
from jax import lax
from jax.sharding import PartitionSpec as P

EXPERTS = 8
SEQ_LEN = 64
loss_scale = 256.0
highest = lax.Precision.HIGHEST


def route_tables(expert_ids, route_share, capacity):
    experts_iota = jnp.arange(EXPERTS, dtype=jnp.int32)
    first_hot = (expert_ids[:, 0:1] == experts_iota[None, :]).astype(jnp.int32)
    second_hot = (expert_ids[:, 1:2] == experts_iota[None, :]).astype(jnp.int32)
    first_rank = jnp.sum((jnp.cumsum(first_hot, axis=0) - first_hot) * first_hot, axis=1)
    second_before = (
        jnp.cumsum(second_hot, axis=0) - second_hot + jnp.sum(first_hot, axis=0)[None, :]
    )
    second_rank = jnp.sum(second_before * second_hot, axis=1)
    route_ranks = jnp.stack([first_rank, second_rank], axis=1)
    route_kept = route_ranks < capacity
    slot_index = jnp.where(route_kept, expert_ids * capacity + route_ranks, -1)
    shares = jnp.stack([route_share, 1.0 - route_share], axis=1) * route_kept.astype(jnp.float32)
    slot_iota = jnp.arange(EXPERTS * capacity, dtype=jnp.int32)
    matches = (slot_index[:, :, None] == slot_iota[None, None, :]).astype(jnp.float32)
    picker = jnp.sum(matches, axis=1)
    mixing = jnp.sum(matches * shares[:, :, None], axis=1)
    return (picker, mixing)


def silu_parts(gate_pre):
    sigmoid_value = jax.nn.sigmoid(gate_pre)
    return (gate_pre * sigmoid_value, sigmoid_value * (1.0 + gate_pre * (1.0 - sigmoid_value)))


def slot_buffer(picker, source_rows, slot_share, replicas, capacity):
    selected = lax.dot_general(
        picker.astype(jnp.bfloat16),
        source_rows,
        (((0,), (0,)), ((), ())),
        preferred_element_type=jnp.float32,
    )
    selected = selected * slot_share[:, None]
    buffer = selected.astype(jnp.bfloat16).reshape(EXPERTS, capacity, source_rows.shape[1])
    return jnp.repeat(buffer, replicas, axis=0)


def gather_slots(picker, source_rows, slot_share, replicas, capacity):
    buffer = slot_buffer(picker, source_rows, slot_share, replicas, capacity)
    arrived = lax.all_to_all(buffer, "ep", split_axis=0, concat_axis=0, tiled=True)
    arrived = lax.all_gather(arrived, "tp", axis=2, tiled=True)
    return arrived.reshape(-1, arrived.shape[2])


def return_sums(term_fn, local_width, replicas, capacity):
    partial_sum = lax.psum_scatter(
        term_fn(jnp.int32(0), lax.axis_size("tp") * local_width).astype(jnp.bfloat16),
        "tp",
        scatter_dimension=0,
        tiled=True,
    ).astype(jnp.float32)
    arrived = lax.all_to_all(
        partial_sum.reshape(local_width, -1, capacity).astype(jnp.bfloat16),
        "ep",
        split_axis=1,
        concat_axis=1,
        tiled=True,
    ).astype(jnp.float32)
    grouped = arrived.reshape(local_width, EXPERTS, replicas, capacity)
    return jnp.sum(grouped, axis=2).reshape(local_width, EXPERTS * capacity)


def per_device(
    tokens, expert_ids, route_share, w_gate, w_up, w_down, reward_head, upstream, pair_order
):
    tok_count, local_width = tokens.shape
    capacity = tok_count * expert_ids.shape[1] // EXPERTS
    replicas = lax.axis_size("ep") // EXPERTS
    picker, mixing = route_tables(expert_ids, route_share, capacity)
    unit_share = jnp.ones((EXPERTS * capacity,), jnp.float32)
    slot_rows = gather_slots(picker, tokens, unit_share, replicas, capacity)
    rows_by_cols = (((1,), (1,)), ((), ()))
    gate_pre = lax.dot_general(slot_rows, w_gate, rows_by_cols, preferred_element_type=jnp.float32)
    up_pre = lax.dot_general(slot_rows, w_up, rows_by_cols, preferred_element_type=jnp.float32)
    silu_value, silu_slope = silu_parts(gate_pre)
    hidden = (silu_value * up_pre).astype(jnp.bfloat16)

    def down_term(first_row, row_count):
        return lax.dot_general(
            w_down, hidden, (((0,), (1,)), ((), ())), preferred_element_type=jnp.float32
        )

    expert_sums = return_sums(down_term, local_width, replicas, capacity)
    mixed_sum = lax.dot_general(
        mixing, expert_sums, rows_by_cols, precision=highest, preferred_element_type=jnp.float32
    )
    layer_out = (tokens.astype(jnp.float32) + mixed_sum).astype(jnp.bfloat16)
    seq_local = tok_count // SEQ_LEN
    seq_total = pair_order.shape[0]
    scores = jnp.dot(layer_out.astype(jnp.float32), reward_head, precision=highest)
    local_rewards = jnp.sum(scores.reshape(seq_local, SEQ_LEN), axis=1) / math.sqrt(SEQ_LEN)
    offset = lax.axis_index("ep") * seq_local
    placed = lax.dynamic_update_slice(
        jnp.zeros((seq_total,), jnp.float32), local_rewards, (offset,)
    )
    rewards = lax.psum(placed, ("ep", "tp"))
    seq_iota = jnp.arange(seq_total, dtype=jnp.int32)
    chosen_hot = (pair_order[0::2][:, None] == seq_iota[None, :]).astype(jnp.float32)
    rejected_hot = (pair_order[1::2][:, None] == seq_iota[None, :]).astype(jnp.float32)
    margin = jnp.dot(chosen_hot, rewards, precision=highest) - jnp.dot(
        rejected_hot, rewards, precision=highest
    )
    pair_loss = jnp.mean(jax.nn.softplus(-margin))
    pair_weight = jax.nn.sigmoid(-margin)
    seq_coef = jnp.dot(pair_weight, rejected_hot - chosen_hot, precision=highest)
    token_coef = jnp.repeat(lax.dynamic_slice_in_dim(seq_coef, offset, seq_local), SEQ_LEN)
    grad_out = (
        upstream.astype(jnp.float32)
        + loss_scale * token_coef[:, None] * reward_head[None, :] / math.sqrt(SEQ_LEN)
    ).astype(jnp.bfloat16)
    slot_share = jnp.sum(mixing, axis=0)
    grad_slots = gather_slots(picker, grad_out, slot_share, replicas, capacity)
    hidden_grad = lax.dot_general(
        grad_slots, w_down, rows_by_cols, preferred_element_type=jnp.float32
    )
    gate_grad = (hidden_grad * up_pre * silu_slope).astype(jnp.bfloat16)
    up_grad = (hidden_grad * silu_value).astype(jnp.bfloat16)
    over_slots = (((0,), (0,)), ((), ()))
    grad_down = lax.dot_general(
        hidden, grad_slots, over_slots, preferred_element_type=jnp.float32
    ).astype(jnp.bfloat16)
    grad_gate = lax.dot_general(
        gate_grad, slot_rows, over_slots, preferred_element_type=jnp.float32
    ).astype(jnp.bfloat16)
    grad_up = lax.dot_general(
        up_grad, slot_rows, over_slots, preferred_element_type=jnp.float32
    ).astype(jnp.bfloat16)

    def input_term(first_row, row_count):
        across = (((0,), (1,)), ((), ()))
        return lax.dot_general(
            w_gate, gate_grad, across, preferred_element_type=jnp.float32
        ) + lax.dot_general(w_up, up_grad, across, preferred_element_type=jnp.float32)

    input_sums = return_sums(input_term, local_width, replicas, capacity)
    returned = lax.dot_general(
        picker, input_sums, rows_by_cols, precision=highest, preferred_element_type=jnp.float32
    )
    grad_tokens = (grad_out.astype(jnp.float32) + returned).astype(jnp.bfloat16)
    return (layer_out, rewards, pair_loss, grad_tokens, grad_gate, grad_up, grad_down)


def solution(mesh):
    in_specs = (
        P("ep", "tp"),
        P("ep", None),
        P("ep"),
        P(("ep", "tp"), None),
        P(("ep", "tp"), None),
        P(("ep", "tp"), None),
        P("tp"),
        P("ep", "tp"),
        P(),
    )
    out_specs = (
        P("ep", "tp"),
        P(),
        P(),
        P("ep", "tp"),
        P(("ep", "tp"), None),
        P(("ep", "tp"), None),
        P(("ep", "tp"), None),
    )
    return jax.shard_map(
        per_device, mesh=mesh, in_specs=in_specs, out_specs=out_specs, check_vma=False
    )
```

profile of v0, /device:TPU:0, one launch (start us, length us, event | category | flops | bytes accessed | tf_op | source)
XLA Modules:
  0.0 279.3 jit_solution(15317795496625174167)
XLA Ops:
  7.2 0.7 subtract_bitcast_fusion
  7.9 0.8 slice_bitcast_fusion.1
  9.4 0.7 add_select_fusion
  10.1 0.7 maximum_select_fusion
  11.0 1.2 convolution_convert_fusion.4
  12.2 19.2 %all_to_all.20 = bf16[8,32,768]{2,1,0:T(8,128)(2,1)} all-to-all(bf16[8,32,768]{2,1,0:T(8,128)(2,1)S(1)} %bitcast.75), channel_id=1, replica_groups=mesh['ep'=8,'tp'=4] {'ep'}, dimensions={0} | all-to-all | bytes 786432 | tf_op jit(solution)/shard_map/all_to_all | solution.py:52
  31.5 18.4 %all-gather.3.cloned.1.call-done = bf16[8,32,3072]{2,1,0:T(8,128)(2,1)} async-done(((bf16[8,32,768]{2,1,0:T(8,128)(2,1)}), bf16[8,32,3072]{2,1,0:T(8,128)(2,1)}) %all-gather.3.cloned.1.call-update) | async-done | bytes 1572880 | tf_op jit(solution)/shard_map/all_gather | solution.py:53
  49.9 8.5 %fusion.30 = f32[256,2048]{1,0:T(8,128)S(1)} fusion(bf16[256,3072]{1,0:T(8,128)(2,1)} %bitcast.67, bf16[2048,3072]{1,0:T(8,128)(2,1)} %param.12), kind=kOutput, calls=%fused_computation.68 | convolution fusion | flops 3221225472 | bytes 16252928 | tf_op jit(solution)/shard_map/dot_general | solution.py:85
  58.5 10.3 %multiply_convert_fusion.2 = (bf16[256,2048]{1,0:T(8,128)(2,1)S(1)}, f32[256,2048]{1,0:T(8,128)}) fusion(f32[256,2048]{1,0:T(8,128)S(1)} %fusion.30, bf16[256,3072]{1,0:T(8,128)(2,1)S(1)} %bitcast.68, bf16[2048,3072]{1,0:T(8,128)(2,1)} %param.13), kind=kOutput, calls=%fused_computation.10 | convolution fusion | flops 3224371200 | bytes 19398656 | tf_op jit(solution)/shard_map/dot_general | solution.py:86
  68.8 1.0 copy-done.2
  69.7 9.1 %fusion.1 = bf16[3072,256]{0,1:T(8,128)(2,1)} fusion(bf16[256,2048]{1,0:T(8,128)(2,1)S(1)} %get-tuple-element.16, bf16[2048,3072]{1,0:T(8,128)(2,1)} %param.14), kind=kOutput, calls=%fused_computation.6 | convolution fusion | flops 3222011904 | bytes 15204352 | tf_op jit(solution)/shard_map/dot_general | solution.py:91
  78.8 28.1 %reduce-scatter.3.cloned.1.call-done = bf16[768,256]{0,1:T(8,128)(2,1)} async-done(((bf16[3072,256]{0,1:T(8,128)(2,1)}), bf16[768,256]{0,1:T(8,128)(2,1)}) %reduce-scatter.3.cloned.1.call-update) | async-done | bytes 393232 | tf_op jit(solution)/shard_map/reduce_scatter | solution.py:58
  107.0 5.5 %all-to-all-start.1 = ((bf16[768,8,32]{0,2,1:T(8,128)(2,1)}), bf16[768,8,32]{0,2,1:T(8,128)(2,1)S(1)}, u32[]{:S(2)}, u32[]{:S(2)}) async-start(bf16[768,8,32]{0,2,1:T(8,128)(2,1)} %bitcast.76), calls=%async_computation.2 | async-start | bytes 786432 | tf_op jit(solution)/shard_map/all_to_all | solution.py:64
  112.6 11.4 %all-to-all-done.1 = bf16[768,8,32]{0,2,1:T(8,128)(2,1)S(1)} async-done(((bf16[768,8,32]{0,2,1:T(8,128)(2,1)}), bf16[768,8,32]{0,2,1:T(8,128)(2,1)S(1)}, u32[]{:S(2)}, u32[]{:S(2)}) %all-to-all-start.1) | async-done | bytes 393248 | tf_op jit(solution)/shard_map/all_to_all | solution.py:64
  124.1 0.3 fusion.5
  125.1 38.5 %psum.7 = f32[16]{0:T(128)S(1)} all-reduce(f32[16]{0:T(128)S(1)} %multiply_dynamic-update-slice_fusion), channel_id=1, replica_groups=mesh['ep'=8,'tp'=4] {'ep','tp'}, use_global_device_ids=true, to_apply=%region_9.10 | all-reduce | flops 16 | bytes 128 | tf_op jit(solution)/shard_map/psum | solution.py:108
  163.8 0.8 fusion.20
  165.1 0.3 fusion.4
  165.4 15.3 %all_to_all.21 = bf16[8,32,768]{2,1,0:T(8,128)(2,1)} all-to-all(bf16[8,32,768]{2,1,0:T(8,128)(2,1)S(1)} %bitcast.78), channel_id=1, replica_groups=mesh['ep'=8,'tp'=4] {'ep'}, dimensions={0} | all-to-all | bytes 786432 | tf_op jit(solution)/shard_map/all_to_all | solution.py:52
  180.8 0.2 reduce-scatter.5.cloned.1.call-start
  181.0 17.7 %all-gather.5.cloned.1.call-done = bf16[8,32,3072]{2,1,0:T(8,128)(2,1)} async-done(((bf16[8,32,768]{2,1,0:T(8,128)(2,1)}), bf16[8,32,3072]{2,1,0:T(8,128)(2,1)}) %all-gather.5.cloned.1.call-update) | async-done | bytes 1572880 | tf_op jit(solution)/shard_map/all_gather | solution.py:53
  198.7 10.2 %multiply_convert_fusion = (bf16[256,2048]{1,0:T(8,128)(2,1)S(1)}, bf16[256,2048]{1,0:T(8,128)(2,1)S(1)}) fusion(f32[256,2048]{1,0:T(8,128)} %copy-done.13, f32[256,2048]{1,0:T(8,128)} %get-tuple-element.17, bf16[256,3072]{1,0:T(8,128)(2,1)} %bitcast.71, bf16[2048,3072]{1,0:T(8,128)(2,1)} %param.14), kind=kOutput, calls=%fused_computation.8 | convolution fusion | flops 3228041216 | bytes 20447232 | tf_op jit(solution)/shard_map/dot_general | solution.py:125
  208.9 7.2 %fusion.31 = f32[256,3072]{1,0:T(8,128)S(1)} fusion(bf16[256,2048]{1,0:T(8,128)(2,1)S(1)} %get-tuple-element.13, bf16[2048,3072]{1,0:T(8,128)(2,1)} %param.12), kind=kOutput, calls=%fused_computation.69 | convolution fusion | flops 3221225472 | bytes 16777216 | tf_op jit(solution)/shard_map/dot_general | solution.py:143
  216.1 9.3 %fusion.2 = bf16[3072,256]{0,1:T(8,128)(2,1)} fusion(f32[256,3072]{1,0:T(8,128)S(1)} %fusion.31, bf16[256,2048]{1,0:T(8,128)(2,1)S(1)} %get-tuple-element.12, bf16[2048,3072]{1,0:T(8,128)(2,1)} %param.13), kind=kOutput, calls=%fused_computation.7 | convolution fusion | flops 3222798336 | bytes 18350080 | tf_op jit(solution)/shard_map/dot_general | solution.py:145
  226.2 0.6 copy-done.1
  226.8 7.9 %convolution_convert_fusion = bf16[2048,3072]{1,0:T(8,128)(2,1)} fusion(bf16[256,2048]{1,0:T(8,128)(2,1)} %copy-done.2, bf16[256,3072]{1,0:T(8,128)(2,1)S(1)} %bitcast.72), kind=kOutput, calls=%fused_computation | convolution fusion | flops 3227516928 | bytes 15204352 | tf_op jit(solution)/shard_map/dot_general | solution.py:131
  234.8 6.6 %convolution_convert_fusion.1 = bf16[2048,3072]{1,0:T(8,128)(2,1)} fusion(bf16[256,2048]{1,0:T(8,128)(2,1)S(1)} %copy-done.6, bf16[256,3072]{1,0:T(8,128)(2,1)S(1)} %bitcast.69), kind=kOutput, calls=%fused_computation.1 | convolution fusion | flops 3227516928 | bytes 15204352 | tf_op jit(solution)/shard_map/dot_general | solution.py:137
  241.4 12.2 %reduce-scatter.5.cloned.1.call-done = bf16[768,256]{0,1:T(8,128)(2,1)} async-done(((bf16[3072,256]{0,1:T(8,128)(2,1)}), bf16[768,256]{0,1:T(8,128)(2,1)}) %reduce-scatter.5.cloned.1.call-update) | async-done | bytes 393232 | tf_op jit(solution)/shard_map/reduce_scatter | solution.py:58
  253.6 5.5 %all-to-all-start.3 = ((bf16[768,8,32]{0,2,1:T(8,128)(2,1)}), bf16[768,8,32]{0,2,1:T(8,128)(2,1)S(1)}, u32[]{:S(2)}, u32[]{:S(2)}) async-start(bf16[768,8,32]{0,2,1:T(8,128)(2,1)} %bitcast.77), calls=%async_computation.5 | async-start | bytes 786432 | tf_op jit(solution)/shard_map/all_to_all | solution.py:64
  259.1 6.6 %convolution_convert_fusion.2 = bf16[2048,3072]{1,0:T(8,128)(2,1)} fusion(bf16[256,2048]{1,0:T(8,128)(2,1)S(1)} %copy-done.4, bf16[256,3072]{1,0:T(8,128)(2,1)S(1)} %bitcast.70), kind=kOutput, calls=%fused_computation.2 | convolution fusion | flops 3227516928 | bytes 15204352 | tf_op jit(solution)/shard_map/dot_general | solution.py:134
  265.7 4.9 %all-to-all-done.3 = bf16[768,8,32]{0,2,1:T(8,128)(2,1)S(1)} async-done(((bf16[768,8,32]{0,2,1:T(8,128)(2,1)}), bf16[768,8,32]{0,2,1:T(8,128)(2,1)S(1)}, u32[]{:S(2)}, u32[]{:S(2)}) %all-to-all-start.3) | async-done | bytes 393248 | tf_op jit(solution)/shard_map/all_to_all | solution.py:64
  270.6 1.0 fusion.6
  (52 shorter events, 2.6 us)
Async XLA Ops:
  7.2 42.8 %all-gather.3.cloned.1.call-start = ((), (), s32[]{:S(2)}) async-start(), calls=%async_computation.6 | async-start | bytes 1966080 | tf_op jit(solution)/shard_map/all_gather | solution.py:53
  31.4 75.6 %reduce-scatter.3.cloned.1.call-start = ((), (), s32[]{:S(2)}) async-start(), calls=%async_computation.7 | async-start | bytes 1966080 | tf_op jit(solution)/shard_map/reduce_scatter | solution.py:58
  49.9 8.6 %copy-start = (bf16[8,32,3072]{2,1,0:T(8,128)(2,1)S(1)}, bf16[8,32,3072]{2,1,0:T(8,128)(2,1)}, u32[]{:S(2)}) copy-start(bf16[8,32,3072]{2,1,0:T(8,128)(2,1)} %all-gather.3.cloned.1.call-done) | copy-start | bytes 4718596
  58.5 10.3 %copy-start.13 = (f32[256,2048]{1,0:T(8,128)}, f32[256,2048]{1,0:T(8,128)S(1)}, u32[]{:S(2)}) copy-start(f32[256,2048]{1,0:T(8,128)S(1)} %fusion.30) | copy-start | bytes 6291460
  68.8 1.0 copy-start.2
  78.8 33.7 %copy-start.11 = (s32[16]{0:T(128)S(1)}, s32[16]{0:T(128)}, u32[]{:S(2)}) copy-start(s32[16]{0:T(128)} %param.17) | copy-start | bytes 196
  78.8 33.8 %copy-start.10 = (f32[768]{0:T(1024)S(1)}, f32[768]{0:T(1024)}, u32[]{:S(2)}) copy-start(f32[768]{0:T(1024)} %param.15) | copy-start | bytes 9220
  78.8 45.2 %copy-start.8 = (bf16[128,768]{1,0:T(8,128)(2,1)S(1)}, bf16[128,768]{1,0:T(8,128)(2,1)}, u32[]{:S(2)}) copy-start(bf16[128,768]{1,0:T(8,128)(2,1)} %param.9) | copy-start | bytes 589828
  78.8 86.3 %copy-start.9 = (bf16[128,768]{1,0:T(8,128)(2,1)S(1)}, bf16[128,768]{1,0:T(8,128)(2,1)}, u32[]{:S(2)}) copy-start(bf16[128,768]{1,0:T(8,128)(2,1)} %param.16) | copy-start | bytes 589828
  107.0 17.1 %all-to-all-start.1 = ((bf16[768,8,32]{0,2,1:T(8,128)(2,1)}), bf16[768,8,32]{0,2,1:T(8,128)(2,1)S(1)}, u32[]{:S(2)}, u32[]{:S(2)}) async-start(bf16[768,8,32]{0,2,1:T(8,128)(2,1)} %bitcast.76), calls=%async_computation.2 | async-start | bytes 786432 | tf_op jit(solution)/shard_map/all_to_all | solution.py:64
  112.5 86.2 %all-gather.5.cloned.1.call-start = ((), (), s32[]{:S(2)}) async-start(), calls=%async_computation.8 | async-start | bytes 1966080 | tf_op jit(solution)/shard_map/all_gather | solution.py:53
  124.4 84.5 %copy-start.7 = (bf16[128,768]{1,0:T(8,128)(2,1)}, bf16[128,768]{1,0:T(8,128)(2,1)S(1)}, u32[]{:S(2)}) copy-start(bf16[128,768]{1,0:T(8,128)(2,1)S(1)} %fusion.5) | copy-start | bytes 589828
  163.6 45.2 %copy-start.12 = (f32[16]{0:T(128)}, f32[16]{0:T(128)S(1)}, u32[]{:S(2)}) copy-start(f32[16]{0:T(128)S(1)} %psum.7) | copy-start | bytes 196
  180.8 72.8 %reduce-scatter.5.cloned.1.call-start = ((), (), s32[]{:S(2)}) async-start(), calls=%async_computation.9 | async-start | bytes 1966080 | tf_op jit(solution)/shard_map/reduce_scatter | solution.py:58
  208.9 7.2 %copy-start.3 = (bf16[256,2048]{1,0:T(8,128)(2,1)}, bf16[256,2048]{1,0:T(8,128)(2,1)S(1)}, u32[]{:S(2)}) copy-start(bf16[256,2048]{1,0:T(8,128)(2,1)S(1)} %get-tuple-element.13) | copy-start | bytes 3145732
  208.9 7.2 %copy-start.5 = (bf16[256,2048]{1,0:T(8,128)(2,1)}, bf16[256,2048]{1,0:T(8,128)(2,1)S(1)}, u32[]{:S(2)}) copy-start(bf16[256,2048]{1,0:T(8,128)(2,1)S(1)} %get-tuple-element.12) | copy-start | bytes 3145732
  225.4 1.4 copy-start.1
  226.8 7.9 %copy-start.6 = (bf16[256,2048]{1,0:T(8,128)(2,1)S(1)}, bf16[256,2048]{1,0:T(8,128)(2,1)}, u32[]{:S(2)}) copy-start(bf16[256,2048]{1,0:T(8,128)(2,1)} %copy-done.5) | copy-start | bytes 3145732
  234.8 24.3 %copy-start.4 = (bf16[256,2048]{1,0:T(8,128)(2,1)S(1)}, bf16[256,2048]{1,0:T(8,128)(2,1)}, u32[]{:S(2)}) copy-start(bf16[256,2048]{1,0:T(8,128)(2,1)} %copy-done.3) | copy-start | bytes 3145732
  253.6 17.0 %all-to-all-start.3 = ((bf16[768,8,32]{0,2,1:T(8,128)(2,1)}), bf16[768,8,32]{0,2,1:T(8,128)(2,1)S(1)}, u32[]{:S(2)}, u32[]{:S(2)}) async-start(bf16[768,8,32]{0,2,1:T(8,128)(2,1)} %bitcast.77), calls=%async_computation.5 | async-start | bytes 786432 | tf_op jit(solution)/shard_map/all_to_all | solution.py:64
Sparse Core Ops, SparseCore 0:
  31.6 18.3 all-gather.2
  79.0 27.9 reduce-scatter.2
  180.9 17.7 all-gather.4
  225.6 27.9 reduce-scatter.4
where the time goes:
time: 280 us; the launch traced here: 279 us
  waiting for transfers between devices  92.9 us (33%)
  matrix products  80 us (29%)
  blocking collectives  73.1 us (26%)
  between operations  15.9 us (6%)
  starting transfers between devices  11.3 us (4%)
  other arithmetic  3.33 us (1%)
  local copies, waits for them, and re-layouts  2.84 us (1%)
    reduce_scatter x2, waiting for transfers between devices, return_sums(): lax.psum_scatter(term_fn(jnp.int32(0), lax.axis_size('tp') * local_width)...  40.3 us
    psum x1, blocking collectives, per_device(): rewards = lax.psum(placed, ('ep', 'tp'))  38.5 us
    all_gather x2, waiting for transfers between devices, gather_slots(): arrived = lax.all_gather(arrived, 'tp', axis=2, tiled=True)  36.1 us
    all_to_all x2, blocking collectives, gather_slots(): lax.all_to_all(buffer, 'ep', split_axis=0, concat_axis=0, tiled=True)  34.5 us
    all_to_all x2, waiting for transfers between devices, return_sums(): lax.all_to_all(partial_sum.reshape(local_width, -1, capacity).astype(jnp....  16.3 us
    all_to_all x2, starting transfers between devices, return_sums(): lax.all_to_all(partial_sum.reshape(local_width, -1, capacity).astype(jnp....  11 us
    dot_general x1, matrix products, per_device(): lax.dot_general(slot_rows, w_up, rows_by_cols, preferred_element_type=jnp...  10.3 us
    dot_general x1, matrix products, per_device(): lax.dot_general(grad_slots, w_down, rows_by_cols, preferred_element_type=...  10.2 us
  transfers between devices with their start and end apart: 6, of which 6 were waited for; matrix products, arithmetic and copies ran while one was open for 8% of the time, Pallas kernels for 0%

commit v1 on v0

--- a/solution.py
+++ b/solution.py
@@ -61,12 +61,20 @@
         scatter_dimension=0,
         tiled=True,
     ).astype(jnp.float32)
-    arrived = lax.all_to_all(
-        partial_sum.reshape(local_width, -1, capacity).astype(jnp.bfloat16),
-        "ep",
-        split_axis=1,
-        concat_axis=1,
-        tiled=True,
+    arrived = jnp.concatenate(
+        lax.all_to_all(
+            jnp.stack(
+                jnp.split(
+                    partial_sum.reshape(local_width, -1, capacity).astype(jnp.bfloat16),
+                    lax.axis_size("ep"),
+                    axis=1,
+                )
+            ),
+            "ep",
+            0,
+            0,
+        ),
+        axis=1,
     ).astype(jnp.float32)
     grouped = arrived.reshape(local_width, EXPERTS, replicas, capacity)
     return jnp.sum(grouped, axis=2).reshape(local_width, EXPERTS * capacity)

time: 280 us -> 304 us (1.086)
  local copies, waits for them, and re-layouts: 2.84 us -> 25.6 us
    unnamed x29 -> x45, local copies, waits for them, and re-layouts: 1.65 us -> 21.5 us
  transfers between devices with their start and end apart: 6 -> 6, of which waited for: 6 -> 6; matrix products, arithmetic and copies ran while one was open for 8% -> 7% of each run, Pallas kernels for 0% -> 0%
where the time goes in v1:
time: 304 us; the launch traced here: 302 us
  waiting for transfers between devices  92.9 us (31%)
  matrix products  80 us (26%)
  blocking collectives  73.1 us (24%)
  local copies, waits for them, and re-layouts  25.6 us (8%)
  between operations  15.9 us (5%)
  starting transfers between devices  11.3 us (4%)
  other arithmetic  3.33 us (1%)
    reduce_scatter x2, waiting for transfers between devices, return_sums(): lax.psum_scatter(term_fn(jnp.int32(0), lax.axis_size('tp') * local_width)...  40.4 us
    psum x1, blocking collectives, per_device(): rewards = lax.psum(placed, ('ep', 'tp'))  38.5 us
    all_gather x2, waiting for transfers between devices, gather_slots(): arrived = lax.all_gather(arrived, 'tp', axis=2, tiled=True)  36.1 us
    all_to_all x2, blocking collectives, gather_slots(): lax.all_to_all(buffer, 'ep', split_axis=0, concat_axis=0, tiled=True)  34.5 us
    unnamed x45, local copies, waits for them, and re-layouts  21.5 us
    all_to_all x2, waiting for transfers between devices, return_sums(): lax.all_to_all(jnp.stack(jnp.split(partial_sum.reshape(local_width, -1, c...  16.3 us
    all_to_all x2, starting transfers between devices, return_sums(): lax.all_to_all(jnp.stack(jnp.split(partial_sum.reshape(local_width, -1, c...  11 us
    dot_general x1, matrix products, per_device(): lax.dot_general(slot_rows, w_up, rows_by_cols, preferred_element_type=jnp...  10.3 us
  transfers between devices with their start and end apart: 6, of which 6 were waited for; matrix products, arithmetic and copies ran while one was open for 7% of the time, Pallas kernels for 0%

profile of v1, /device:TPU:0, one launch (start us, length us, event | category | flops | bytes accessed | tf_op | source)
XLA Modules:
  0.0 302.1 jit_solution(14353594832376451544)
XLA Ops:
  12.2 19.2 %all_to_all.20 = bf16[8,32,768]{2,1,0:T(8,128)(2,1)} all-to-all(bf16[8,32,768]{2,1,0:T(8,128)(2,1)S(1)} %bitcast.143), channel_id=1, replica_groups=mesh['ep'=8,'tp'=4] {'ep'}, dimensions={0} | all-to-all | bytes 786432 | tf_op jit(solution)/shard_map/all_to_all | solution.py:52
  31.5 18.4 %all-gather.3.cloned.1.call-done = bf16[8,32,3072]{2,1,0:T(8,128)(2,1)} async-done(((bf16[8,32,768]{2,1,0:T(8,128)(2,1)}), bf16[8,32,3072]{2,1,0:T(8,128)(2,1)}) %all-gather.3.cloned.1.call-update) | async-done | bytes 1572880 | tf_op jit(solution)/shard_map/all_gather | solution.py:53
  49.9 8.5 %fusion.46 = f32[256,2048]{1,0:T(8,128)S(1)} fusion(bf16[256,3072]{1,0:T(8,128)(2,1)} %bitcast.135, bf16[2048,3072]{1,0:T(8,128)(2,1)} %param.12), kind=kOutput, calls=%fused_computation.100 | convolution fusion | flops 3221225472 | bytes 16252928 | tf_op jit(solution)/shard_map/dot_general | solution.py:93
  58.5 10.3 %multiply_convert_fusion.2 = (bf16[256,2048]{1,0:T(8,128)(2,1)S(1)}, f32[256,2048]{1,0:T(8,128)}) fusion(f32[256,2048]{1,0:T(8,128)S(1)} %fusion.46, bf16[256,3072]{1,0:T(8,128)(2,1)S(1)} %bitcast.136, bf16[2048,3072]{1,0:T(8,128)(2,1)} %param.13), kind=kOutput, calls=%fused_computation.10 | convolution fusion | flops 3224371200 | bytes 19398656 | tf_op jit(solution)/shard_map/dot_general | solution.py:94
  69.8 9.1 %fusion.1 = bf16[3072,256]{0,1:T(8,128)(2,1)} fusion(bf16[256,2048]{1,0:T(8,128)(2,1)S(1)} %get-tuple-element.16, bf16[2048,3072]{1,0:T(8,128)(2,1)} %param.14), kind=kOutput, calls=%fused_computation.6 | convolution fusion | flops 3222011904 | bytes 15204352 | tf_op jit(solution)/shard_map/dot_general | solution.py:99
  78.9 28.1 %reduce-scatter.3.cloned.1.call-done = bf16[768,256]{0,1:T(8,128)(2,1)} async-done(((bf16[3072,256]{0,1:T(8,128)(2,1)}), bf16[768,256]{0,1:T(8,128)(2,1)}) %reduce-scatter.3.cloned.1.call-update) | async-done | bytes 393232 | tf_op jit(solution)/shard_map/reduce_scatter | solution.py:58
  107.0 1.4 fusion.26
  108.4 1.4 fusion.25
  109.9 1.4 fusion.24
  111.3 1.4 fusion.23
  112.7 1.4 fusion.22
  114.1 1.4 fusion.21
  115.6 1.4 fusion.20
  117.0 1.4 fusion.19
  118.4 5.5 %all-to-all-start.1 = ((bf16[8,768,1,32]{1,3,2,0:T(8,128)(2,1)}), bf16[8,768,1,32]{1,3,2,0:T(8,128)(2,1)S(1)}, u32[]{:S(2)}, u32[]{:S(2)}) async-start(bf16[8,768,1,32]{1,3,2,0:T(8,128)(2,1)} %fusion.19), calls=%async_computation.2 | async-start | bytes 786432 | tf_op jit(solution)/shard_map/all_to_all | solution.py:65
  124.1 11.4 %all-to-all-done.1 = bf16[8,768,1,32]{1,3,2,0:T(8,128)(2,1)S(1)} async-done(((bf16[8,768,1,32]{1,3,2,0:T(8,128)(2,1)}), bf16[8,768,1,32]{1,3,2,0:T(8,128)(2,1)S(1)}, u32[]{:S(2)}, u32[]{:S(2)}) %all-to-all-start.1) | async-done | bytes 393248 | tf_op jit(solution)/shard_map/all_to_all | solution.py:65
  136.5 38.5 %psum.7 = f32[16]{0:T(128)S(1)} all-reduce(f32[16]{0:T(128)S(1)} %multiply_dynamic-update-slice_fusion), channel_id=1, replica_groups=mesh['ep'=8,'tp'=4] {'ep','tp'}, use_global_device_ids=true, to_apply=%region_9.10 | all-reduce | flops 16 | bytes 128 | tf_op jit(solution)/shard_map/psum | solution.py:116
  176.8 15.3 %all_to_all.21 = bf16[8,32,768]{2,1,0:T(8,128)(2,1)} all-to-all(bf16[8,32,768]{2,1,0:T(8,128)(2,1)S(1)} %bitcast.160), channel_id=1, replica_groups=mesh['ep'=8,'tp'=4] {'ep'}, dimensions={0} | all-to-all | bytes 786432 | tf_op jit(solution)/shard_map/all_to_all | solution.py:52
  192.4 17.7 %all-gather.5.cloned.1.call-done = bf16[8,32,3072]{2,1,0:T(8,128)(2,1)} async-done(((bf16[8,32,768]{2,1,0:T(8,128)(2,1)}), bf16[8,32,3072]{2,1,0:T(8,128)(2,1)}) %all-gather.5.cloned.1.call-update) | async-done | bytes 1572880 | tf_op jit(solution)/shard_map/all_gather | solution.py:53
  210.1 10.2 %multiply_convert_fusion = (bf16[256,2048]{1,0:T(8,128)(2,1)S(1)}, bf16[256,2048]{1,0:T(8,128)(2,1)S(1)}) fusion(f32[256,2048]{1,0:T(8,128)} %copy-done.14, f32[256,2048]{1,0:T(8,128)} %get-tuple-element.17, bf16[256,3072]{1,0:T(8,128)(2,1)} %bitcast.139, bf16[2048,3072]{1,0:T(8,128)(2,1)} %param.14), kind=kOutput, calls=%fused_computation.8 | convolution fusion | flops 3228041216 | bytes 20447232 | tf_op jit(solution)/shard_map/dot_general | solution.py:133
  220.3 7.2 %fusion.47 = f32[256,3072]{1,0:T(8,128)S(1)} fusion(bf16[256,2048]{1,0:T(8,128)(2,1)S(1)} %get-tuple-element.13, bf16[2048,3072]{1,0:T(8,128)(2,1)} %param.12), kind=kOutput, calls=%fused_computation.101 | convolution fusion | flops 3221225472 | bytes 16777216 | tf_op jit(solution)/shard_map/dot_general | solution.py:151
  227.5 9.3 %fusion.2 = bf16[3072,256]{0,1:T(8,128)(2,1)} fusion(f32[256,3072]{1,0:T(8,128)S(1)} %fusion.47, bf16[256,2048]{1,0:T(8,128)(2,1)S(1)} %get-tuple-element.12, bf16[2048,3072]{1,0:T(8,128)(2,1)} %param.13), kind=kOutput, calls=%fused_computation.7 | convolution fusion | flops 3222798336 | bytes 18350080 | tf_op jit(solution)/shard_map/dot_general | solution.py:153
  238.2 7.9 %convolution_convert_fusion = bf16[2048,3072]{1,0:T(8,128)(2,1)} fusion(bf16[256,2048]{1,0:T(8,128)(2,1)} %copy-done.2, bf16[256,3072]{1,0:T(8,128)(2,1)S(1)} %bitcast.140), kind=kOutput, calls=%fused_computation | convolution fusion | flops 3227516928 | bytes 15204352 | tf_op jit(solution)/shard_map/dot_general | solution.py:139
  246.2 6.6 %convolution_convert_fusion.1 = bf16[2048,3072]{1,0:T(8,128)(2,1)} fusion(bf16[256,2048]{1,0:T(8,128)(2,1)S(1)} %copy-done.6, bf16[256,3072]{1,0:T(8,128)(2,1)S(1)} %bitcast.137), kind=kOutput, calls=%fused_computation.1 | convolution fusion | flops 3227516928 | bytes 15204352 | tf_op jit(solution)/shard_map/dot_general | solution.py:145
  252.8 12.2 %reduce-scatter.5.cloned.1.call-done = bf16[768,256]{0,1:T(8,128)(2,1)} async-done(((bf16[3072,256]{0,1:T(8,128)(2,1)}), bf16[768,256]{0,1:T(8,128)(2,1)}) %reduce-scatter.5.cloned.1.call-update) | async-done | bytes 393232 | tf_op jit(solution)/shard_map/reduce_scatter | solution.py:58
  267.8 1.4 fusion.16
  270.7 1.4 fusion.14
  273.5 1.4 fusion.12
  274.9 1.4 fusion.11
  276.3 5.5 %all-to-all-start.3 = ((bf16[8,768,1,32]{1,3,2,0:T(8,128)(2,1)}), bf16[8,768,1,32]{1,3,2,0:T(8,128)(2,1)S(1)}, u32[]{:S(2)}, u32[]{:S(2)}) async-start(bf16[8,768,1,32]{1,3,2,0:T(8,128)(2,1)} %fusion.11), calls=%async_computation.5 | async-start | bytes 786432 | tf_op jit(solution)/shard_map/all_to_all | solution.py:65
  281.8 6.6 %convolution_convert_fusion.2 = bf16[2048,3072]{1,0:T(8,128)(2,1)} fusion(bf16[256,2048]{1,0:T(8,128)(2,1)S(1)} %copy-done.4, bf16[256,3072]{1,0:T(8,128)(2,1)S(1)} %bitcast.138), kind=kOutput, calls=%fused_computation.2 | convolution fusion | flops 3227516928 | bytes 15204352 | tf_op jit(solution)/shard_map/dot_general | solution.py:142
  288.5 4.9 %all-to-all-done.3 = bf16[8,768,1,32]{1,3,2,0:T(8,128)(2,1)S(1)} async-done(((bf16[8,768,1,32]{1,3,2,0:T(8,128)(2,1)}), bf16[8,768,1,32]{1,3,2,0:T(8,128)(2,1)S(1)}, u32[]{:S(2)}, u32[]{:S(2)}) %all-to-all-start.3) | async-done | bytes 393248 | tf_op jit(solution)/shard_map/all_to_all | solution.py:65
  (70 shorter events, 16.6 us)
Async XLA Ops:
  7.2 42.8 %all-gather.3.cloned.1.call-start = ((), (), s32[]{:S(2)}) async-start(), calls=%async_computation.6 | async-start | bytes 1966080 | tf_op jit(solution)/shard_map/all_gather | solution.py:53
  31.4 75.6 %reduce-scatter.3.cloned.1.call-start = ((), (), s32[]{:S(2)}) async-start(), calls=%async_computation.7 | async-start | bytes 1966080 | tf_op jit(solution)/shard_map/reduce_scatter | solution.py:58
  49.9 8.6 %copy-start = (bf16[8,32,3072]{2,1,0:T(8,128)(2,1)S(1)}, bf16[8,32,3072]{2,1,0:T(8,128)(2,1)}, u32[]{:S(2)}) copy-start(bf16[8,32,3072]{2,1,0:T(8,128)(2,1)} %all-gather.3.cloned.1.call-done) | copy-start | bytes 4718596
  58.5 10.3 %copy-start.14 = (f32[256,2048]{1,0:T(8,128)}, f32[256,2048]{1,0:T(8,128)S(1)}, u32[]{:S(2)}) copy-start(f32[256,2048]{1,0:T(8,128)S(1)} %fusion.46) | copy-start | bytes 6291460
  68.8 1.0 copy-start.2
  78.8 45.1 %copy-start.12 = (s32[16]{0:T(128)S(1)}, s32[16]{0:T(128)}, u32[]{:S(2)}) copy-start(s32[16]{0:T(128)} %param.17) | copy-start | bytes 196
  78.8 45.2 %copy-start.11 = (f32[768]{0:T(1024)S(1)}, f32[768]{0:T(1024)}, u32[]{:S(2)}) copy-start(f32[768]{0:T(1024)} %param.15) | copy-start | bytes 9220
  78.8 56.6 %copy-start.8 = (bf16[128,768]{1,0:T(8,128)(2,1)S(1)}, bf16[128,768]{1,0:T(8,128)(2,1)}, u32[]{:S(2)}) copy-start(bf16[128,768]{1,0:T(8,128)(2,1)} %param.9) | copy-start | bytes 589828
  78.8 97.6 %copy-start.9 = (bf16[128,768]{1,0:T(8,128)(2,1)S(1)}, bf16[128,768]{1,0:T(8,128)(2,1)}, u32[]{:S(2)}) copy-start(bf16[128,768]{1,0:T(8,128)(2,1)} %param.16) | copy-start | bytes 589828
  118.4 17.1 %all-to-all-start.1 = ((bf16[8,768,1,32]{1,3,2,0:T(8,128)(2,1)}), bf16[8,768,1,32]{1,3,2,0:T(8,128)(2,1)S(1)}, u32[]{:S(2)}, u32[]{:S(2)}) async-start(bf16[8,768,1,32]{1,3,2,0:T(8,128)(2,1)} %fusion.19), calls=%async_computation.2 | async-start | bytes 786432 | tf_op jit(solution)/shard_map/all_to_all | solution.py:65
  123.9 86.2 %all-gather.5.cloned.1.call-start = ((), (), s32[]{:S(2)}) async-start(), calls=%async_computation.8 | async-start | bytes 1966080 | tf_op jit(solution)/shard_map/all_gather | solution.py:53
  135.8 84.5 %copy-start.7 = (bf16[128,768]{1,0:T(8,128)(2,1)}, bf16[128,768]{1,0:T(8,128)(2,1)S(1)}, u32[]{:S(2)}) copy-start(bf16[128,768]{1,0:T(8,128)(2,1)S(1)} %fusion.5) | copy-start | bytes 589828
  175.0 45.2 %copy-start.13 = (f32[16]{0:T(128)}, f32[16]{0:T(128)S(1)}, u32[]{:S(2)}) copy-start(f32[16]{0:T(128)S(1)} %psum.7) | copy-start | bytes 196
  192.2 72.8 %reduce-scatter.5.cloned.1.call-start = ((), (), s32[]{:S(2)}) async-start(), calls=%async_computation.9 | async-start | bytes 1966080 | tf_op jit(solution)/shard_map/reduce_scatter | solution.py:58
  220.3 7.2 %copy-start.3 = (bf16[256,2048]{1,0:T(8,128)(2,1)}, bf16[256,2048]{1,0:T(8,128)(2,1)S(1)}, u32[]{:S(2)}) copy-start(bf16[256,2048]{1,0:T(8,128)(2,1)S(1)} %get-tuple-element.13) | copy-start | bytes 3145732
  220.3 7.2 %copy-start.5 = (bf16[256,2048]{1,0:T(8,128)(2,1)}, bf16[256,2048]{1,0:T(8,128)(2,1)S(1)}, u32[]{:S(2)}) copy-start(bf16[256,2048]{1,0:T(8,128)(2,1)S(1)} %get-tuple-element.12) | copy-start | bytes 3145732
  236.8 1.4 copy-start.1
  238.2 7.9 %copy-start.6 = (bf16[256,2048]{1,0:T(8,128)(2,1)S(1)}, bf16[256,2048]{1,0:T(8,128)(2,1)}, u32[]{:S(2)}) copy-start(bf16[256,2048]{1,0:T(8,128)(2,1)} %copy-done.5) | copy-start | bytes 3145732
  252.8 29.1 %copy-start.4 = (bf16[256,2048]{1,0:T(8,128)(2,1)S(1)}, bf16[256,2048]{1,0:T(8,128)(2,1)}, u32[]{:S(2)}) copy-start(bf16[256,2048]{1,0:T(8,128)(2,1)} %copy-done.3) | copy-start | bytes 3145732
  276.3 17.1 %all-to-all-start.3 = ((bf16[8,768,1,32]{1,3,2,0:T(8,128)(2,1)}), bf16[8,768,1,32]{1,3,2,0:T(8,128)(2,1)S(1)}, u32[]{:S(2)}, u32[]{:S(2)}) async-start(bf16[8,768,1,32]{1,3,2,0:T(8,128)(2,1)} %fusion.11), calls=%async_computation.5 | async-start | bytes 786432 | tf_op jit(solution)/shard_map/all_to_all | solution.py:65
  281.8 11.6 %copy-start.10 = (bf16[128,768]{1,0:T(8,128)(2,1)S(1)}, bf16[128,768]{1,0:T(8,128)(2,1)}, u32[]{:S(2)}) copy-start(bf16[128,768]{1,0:T(8,128)(2,1)} %param.16) | copy-start | bytes 589828
Sparse Core Ops, SparseCore 0:
  31.6 18.3 all-gather.2
  79.0 27.9 reduce-scatter.2
  192.3 17.7 all-gather.4
  236.9 28.0 reduce-scatter.4
